TPU v7x, 32 devices: a whole 2x2x4 slice. The times are simulated.
32 devices in a mesh: seg: 4 (over y, x), lat: 8 (over z, core).
Axes of the slice: x: 2, y: 2, z: 4, core: 2. Of those that a mesh axis runs over, the one named last changes fastest.
Arguments:
- coh_map: bfloat16 [4, 65536, 128], P('seg', 'lat'), may hold values from 0 to 40, as said below
- positions: int32 [4, 1024], P('seg', 'lat'), may hold values from 0 to 16776959, as said below
- counts: int32 [16], P('lat'), may hold values from 1 to 64, as said below
Outputs:
- semi_stat: bfloat16 [1024, 128], P('lat')
- excess: float32 [16, 128], P('lat')
Inputs may be any that keep to these rules, and one draw needn't show every extreme that they name: `coh_map`: nonnegative. `counts`: the first block has 1 valid point and the last block 64. `positions`: the bins are split into 8 aligned slices of 8192 bins; a point's two bins lie in the same slice; in each segment, at most 32 of the 128 points of one index of lat have their bins in one slice, and that most is reached in every draw.
All inputs are finite; a program needn't handle non-finite values.
Results may differ from a plain program's by a relative error of at most 0.001.
Values sent between devices are 32-bit elements; how exact they have to be, the bound alone decides.
A program may use at most 64 MiB of HBM per device.

v0:
```python
import jax
import jax.numpy as jnp
from jax import lax
from jax.sharding import PartitionSpec as P


def routed_sums(positions, coh_map, first_bin):
    seg_count = coh_map.shape[0]
    slice_bins = coh_map.shape[1]
    width = coh_map.shape[2]
    own_rows = positions.shape[1]
    n_lataxis = lax.axis_size("lat")
    slot_limit = 2 * own_rows // n_lataxis
    dest = positions // 256 // slice_bins
    dest_hits = (dest[:, :, None] == lax.broadcasted_iota(jnp.int32, (1, 1, n_lataxis), 2)).astype(
        jnp.int32
    )
    before = jnp.cumsum(dest_hits, axis=1) - dest_hits
    slot = jnp.sum(before * dest_hits, axis=2)
    seg_ids = lax.broadcasted_iota(jnp.int32, positions.shape, 0)
    outgoing = (
        jnp.full((n_lataxis, seg_count, slot_limit), -1, jnp.int32)
        .at[dest, seg_ids, slot]
        .set(positions)
    )
    bin_index = lax.broadcasted_iota(jnp.int32, (1, slice_bins), 1)
    incoming = lax.all_to_all(outgoing, "lat", split_axis=0, concat_axis=0, tiled=True)
    item_count = incoming.shape[2]
    pos_flat = incoming[:, 0, :].reshape(-1)
    live = (pos_flat >= 0)[:, None]
    rel_bin = (pos_flat // 256 - first_bin)[:, None]
    fraction = (pos_flat % 256).astype(jnp.float32)[:, None] / 256.0
    weights = jnp.where(live & (bin_index == rel_bin), 1.0 - fraction, 0.0) + jnp.where(
        live & (bin_index == rel_bin + 1), fraction, 0.0
    )
    rows = jnp.dot(weights.astype(jnp.bfloat16), coh_map[0], preferred_element_type=jnp.float32)
    row_list = [rows.reshape(n_lataxis, item_count, width)]
    stacked = jnp.stack(row_list, axis=1)
    returned = lax.all_to_all(stacked, "lat", split_axis=0, concat_axis=0, tiled=True)
    by_segment = returned.transpose(1, 0, 2, 3).reshape(seg_count, n_lataxis * slot_limit, width)
    flat_index = dest * slot_limit + slot
    picked = jnp.take_along_axis(by_segment, flat_index[:, :, None], axis=1)
    return jnp.sum(picked, axis=0)


def shards(coh_map, positions, counts):
    seg_count = coh_map.shape[0]
    slice_bins = coh_map.shape[1]
    first_bin = lax.axis_index("lat") * slice_bins
    n_segaxis = lax.axis_size("seg")
    total_segs = seg_count * n_segaxis
    own_rows = positions.shape[1]
    local_sums_rows = routed_sums(positions, coh_map, first_bin)
    summed = lax.psum(local_sums_rows, "seg")
    semi_stat = summed / total_segs
    block_count = counts.shape[0]
    block_size = own_rows // block_count
    grouped = semi_stat.reshape(block_count, block_size, semi_stat.shape[1])
    slot_index = lax.broadcasted_iota(jnp.int32, (block_count, block_size, 1), 1)
    live_mask = slot_index < counts[:, None, None]
    block_sums = jnp.sum(jnp.where(live_mask, grouped, 0.0), axis=1)
    count_float = counts.astype(jnp.float32)
    block_means = block_sums / count_float[:, None]
    column_sums, total_count = lax.psum((jnp.sum(block_sums, axis=0), jnp.sum(count_float)), "lat")
    global_mean = column_sums / total_count
    excess = block_means - global_mean[None, :]
    return (semi_stat.astype(jnp.bfloat16), excess)


def solution(mesh):
    in_specs = (P("seg", "lat", None), P("seg", "lat"), P("lat"))
    out_specs = (P("lat", None), P("lat", None))
    return jax.shard_map(shards, mesh=mesh, in_specs=in_specs, out_specs=out_specs, check_vma=False)
```

profile of v0, /device:TPU:0, one launch (start us, length us, event | category | flops | bytes accessed | tf_op | source)
XLA Modules:
  0.0 125.4 jit_solution(7126655053401794815)
XLA Ops:
  7.2 0.0 copy-start
  7.2 0.8 fusion.19
  8.0 0.1 fusion.12
  8.1 0.2 reduce_window_sum.11
  8.3 0.2 select_reduce_fusion.2
  8.5 0.6 broadcast.427
  9.1 19.9 %scatter_fusion = s32[8,32]{1,0:T(8,128)} fusion(s32[8,32]{1,0:T(8,128)} %broadcast.427, s32[128]{0:T(128)S(1)} %fusion.21, s32[128]{0:T(128)} %bitcast.50), kind=kCustom, calls=%fused_computation.1 | custom fusion | bytes 2560 | tf_op jit(solution)/shard_map/scatter | solution.py:24
  29.0 6.4 %all-to-all-start = ((s32[8,1,32]{2,1,0:T(1,128)}), s32[8,1,32]{2,1,0:T(1,128)S(1)}, u32[]{:S(2)}, u32[]{:S(2)}) async-start(s32[8,1,32]{2,1,0:T(1,128)} %bitcast.9), calls=%async_computation | async-start | bytes 8192 | tf_op jit(solution)/shard_map/all_to_all | solution.py:27
  35.3 0.7 iota_compare_fusion.3
  36.0 4.8 %all-to-all-done = s32[8,1,32]{2,1,0:T(1,128)S(1)} async-done(((s32[8,1,32]{2,1,0:T(1,128)}), s32[8,1,32]{2,1,0:T(1,128)S(1)}, u32[]{:S(2)}, u32[]{:S(2)}) %all-to-all-start) | async-done | bytes 1056 | tf_op jit(solution)/shard_map/all_to_all | solution.py:27
  40.9 0.0 copy-done
  40.9 0.0 copy-start.1
  40.9 5.0 %fusion.7 = f32[8,1,32,128]{3,2,1,0:T(8,128)} fusion(bf16[1,8192,128]{2,1,0:T(8,128)(2,1)S(1)} %copy-done, f32[8,32]{1,0:T(8,128)S(1)} %get-tuple-element.5, s32[8,32]{1,0:T(8,128)S(1)} %get-tuple-element.6, f32[8,32]{1,0:T(8,128)S(1)} %get-tuple-element.4, s32[8,32]{1,0:T(8,128)S(1)} %get-tuple-element.7, pred[8,32]{1,0:T(8,128)(4,1)S(1)} %broadcast_compare_fusion), kind=kOutput, calls=%fused_computation.11 | convolution fusion | flops 553648128 | bytes 2232576 | tf_op jit(solution)/shard_map/dot_general | solution.py:36
  45.9 3.4 %all-to-all-start.1 = ((f32[8,1,32,128]{3,2,1,0:T(8,128)}), f32[8,1,32,128]{3,2,1,0:T(8,128)S(1)}, u32[]{:S(2)}, u32[]{:S(2)}) async-start(f32[8,1,32,128]{3,2,1,0:T(8,128)} %fusion.7), calls=%async_computation.1 | async-start | bytes 262144 | tf_op jit(solution)/shard_map/all_to_all | solution.py:39
  49.2 0.0 all-reduce.3.cloned.1.call-start
  49.3 0.0 copy-done.1
  49.3 0.1 lt.77
  49.4 6.5 %all-to-all-done.1 = f32[8,1,32,128]{3,2,1,0:T(8,128)S(1)} async-done(((f32[8,1,32,128]{3,2,1,0:T(8,128)}), f32[8,1,32,128]{3,2,1,0:T(8,128)S(1)}, u32[]{:S(2)}, u32[]{:S(2)}) %all-to-all-start.1) | async-done | bytes 131104 | tf_op jit(solution)/shard_map/all_to_all | solution.py:39
  55.9 0.6 gather_fusion
  56.6 0.7 broadcast_select_fusion
  57.3 0.0 all-reduce.3.cloned.1.call-update
  57.3 0.6 convert_reduce_fusion
  57.9 40.4 %all-reduce.3.cloned.1.call-done = f32[128,128]{1,0:T(8,128)} async-done(((f32[128,128]{1,0:T(8,128)}), f32[128,128]{1,0:T(8,128)}) %all-reduce.3.cloned.1.call-update) | async-done | bytes 65552 | tf_op jit(solution)/shard_map/psum | solution.py:54
  98.3 1.5 %select_reduce_fusion = (f32[128]{0:T(128)S(1)}, bf16[128,128]{1,0:T(8,128)(2,1)}) fusion(pred[128]{0:T(512)(128)(4,1)S(1)} %lt.77, f32[128,128]{1,0:T(8,128)} %all-reduce.3.cloned.1.call-done), kind=kLoop, calls=%fused_computation.12 | loop fusion | flops 65408 | bytes 98944 | tf_op jit(solution)/shard_map/reduce_sum | solution.py:64
  99.8 16.6 %all-reduce = (f32[128]{0:T(128)S(1)}, f32[]{:T(128)}) all-reduce(f32[128]{0:T(128)S(1)} %get-tuple-element.10, f32[]{:T(128)} %convert_reduce_fusion), channel_id=1, replica_groups=mesh['seg'=4,'lat'=8] {'lat'}, use_global_device_ids=true, to_apply=%region_6.7 | all-reduce | flops 129 | bytes 1032 | tf_op jit(solution)/shard_map/psum | solution.py:64
  116.3 0.6 broadcast_divide_fusion
  117.0 0.9 select_reduce_fusion.1
  117.9 0.6 divide_subtract_fusion
  (11 shorter events, 0.1 us)
Async XLA Ops:
  7.2 33.7 %copy-start = (bf16[1,8192,128]{2,1,0:T(8,128)(2,1)S(1)}, bf16[1,8192,128]{2,1,0:T(8,128)(2,1)}, u32[]{:S(2)}) copy-start(bf16[1,8192,128]{2,1,0:T(8,128)(2,1)} %param.3) | copy-start | bytes 6291460
  29.0 11.9 %all-to-all-start = ((s32[8,1,32]{2,1,0:T(1,128)}), s32[8,1,32]{2,1,0:T(1,128)S(1)}, u32[]{:S(2)}, u32[]{:S(2)}) async-start(s32[8,1,32]{2,1,0:T(1,128)} %bitcast.9), calls=%async_computation | async-start | bytes 8192 | tf_op jit(solution)/shard_map/all_to_all | solution.py:27
  40.9 8.4 %copy-start.1 = (s32[2]{0:T(128)S(1)}, s32[2]{0:T(128)}, u32[]{:S(2)}) copy-start(s32[2]{0:T(128)} %param.5) | copy-start | bytes 28
  45.9 10.1 %all-to-all-start.1 = ((f32[8,1,32,128]{3,2,1,0:T(8,128)}), f32[8,1,32,128]{3,2,1,0:T(8,128)S(1)}, u32[]{:S(2)}, u32[]{:S(2)}) async-start(f32[8,1,32,128]{3,2,1,0:T(8,128)} %fusion.7), calls=%async_computation.1 | async-start | bytes 262144 | tf_op jit(solution)/shard_map/all_to_all | solution.py:39
  49.2 49.1 %all-reduce.3.cloned.1.call-start = ((), (), s32[]{:S(2)}) async-start(), calls=%async_computation.2 | async-start | bytes 131072 | tf_op jit(solution)/shard_map/psum | solution.py:54
Sparse Core Ops, SparseCore 0:
  57.4 40.8 all-reduce.2
where the time goes:
time: 126 us; the launch traced here: 125 us
  waiting for transfers between devices  51.7 us (41%)
  local copies, waits for them, and re-layouts  21.2 us (17%)
  blocking collectives  16.6 us (13%)
  between operations  14.1 us (11%)
  starting transfers between devices  9.76 us (8%)
  other arithmetic  7.05 us (6%)
  matrix products  4.96 us (4%)
    psum x1, waiting for transfers between devices, shards(): summed = lax.psum(local_sums_rows, 'seg')  40.4 us
    scatter x1, local copies, waits for them, and re-layouts, routed_sums(): outgoing = jnp.full((n_lataxis, seg_count, slot_limit), -1, jnp.int32).at...  19.9 us
    psum x1, blocking collectives, shards(): lax.psum((jnp.sum(block_sums, axis=0), jnp.sum(count_float)), 'lat')  16.6 us
    all_to_all x1, waiting for transfers between devices, routed_sums(): lax.all_to_all(stacked, 'lat', split_axis=0, concat_axis=0, tiled=True)  6.51 us
    all_to_all x1, starting transfers between devices, routed_sums(): lax.all_to_all(outgoing, 'lat', split_axis=0, concat_axis=0, tiled=True)  6.35 us
    dot_general x1, matrix products, routed_sums(): jnp.dot(weights.astype(jnp.bfloat16), coh_map[0], preferred_element_type=...  4.96 us
    all_to_all x1, waiting for transfers between devices, routed_sums(): lax.all_to_all(outgoing, 'lat', split_axis=0, concat_axis=0, tiled=True)  4.77 us
    all_to_all x1, starting transfers between devices, routed_sums(): lax.all_to_all(stacked, 'lat', split_axis=0, concat_axis=0, tiled=True)  3.37 us
  transfers between devices with their start and end apart: 3, of which 3 were waited for; matrix products, arithmetic and copies ran while one was open for 1% of the time, Pallas kernels for 0%

commit v1 on v0

--- a/solution.py
+++ b/solution.py
@@ -51,7 +51,8 @@
     total_segs = seg_count * n_segaxis
     own_rows = positions.shape[1]
     local_sums_rows = routed_sums(positions, coh_map, first_bin)
-    summed = lax.psum(local_sums_rows, "seg")
+    blocks = lax.all_gather(local_sums_rows, "seg", axis=0, tiled=False)
+    summed = blocks.sum(axis=0)
     semi_stat = summed / total_segs
     block_count = counts.shape[0]
     block_size = own_rows // block_count

time: 126 us -> 76.1 us (0.60)
  waiting for transfers between devices: 51.7 us -> 10.7 us
  between operations: 14.1 us -> 0.75 us
  blocking collectives: 16.6 us -> 23.2 us
  other arithmetic: 7.05 us -> 4.77 us
    psum x1 -> x0, waiting for transfers between devices: 40.4 us -> none  [shards(): summed = lax.psum(local_sums_rows, 'seg')]
    all_gather x0 -> x1, blocking collectives: none -> 8.99 us  [shards(): blocks = lax.all_gather(local_sums_rows, 'seg', axis=0, tiled=False)]
    psum x1, blocking collectives: 16.6 us -> 14.2 us  [shards(): lax.psum((jnp.sum(block_sums, axis=0), jnp.sum(count_float)), 'lat')]
  transfers between devices with their start and end apart: 3 -> 2, of which waited for: 3 -> 2; matrix products, arithmetic and copies ran while one was open for 1% -> 2% of each run, Pallas kernels for 0% -> 0%
where the time goes in v1:
time: 76.1 us; the launch traced here: 75.4 us
  blocking collectives  23.2 us (30%)
  local copies, waits for them, and re-layouts  21.2 us (28%)
  waiting for transfers between devices  10.7 us (14%)
  starting transfers between devices  9.72 us (13%)
  matrix products  4.96 us (7%)
  other arithmetic  4.77 us (6%)
    scatter x1, local copies, waits for them, and re-layouts, routed_sums(): outgoing = jnp.full((n_lataxis, seg_count, slot_limit), -1, jnp.int32).at...  19.9 us
    psum x1, blocking collectives, shards(): lax.psum((jnp.sum(block_sums, axis=0), jnp.sum(count_float)), 'lat')  14.2 us
    all_gather x1, blocking collectives, shards(): blocks = lax.all_gather(local_sums_rows, 'seg', axis=0, tiled=False)  8.99 us
    all_to_all x1, starting transfers between devices, routed_sums(): lax.all_to_all(outgoing, 'lat', split_axis=0, concat_axis=0, tiled=True)  6.35 us
    all_to_all x1, waiting for transfers between devices, routed_sums(): lax.all_to_all(stacked, 'lat', split_axis=0, concat_axis=0, tiled=True)  5.98 us
    dot_general x1, matrix products, routed_sums(): jnp.dot(weights.astype(jnp.bfloat16), coh_map[0], preferred_element_type=...  4.96 us
    all_to_all x1, waiting for transfers between devices, routed_sums(): lax.all_to_all(outgoing, 'lat', split_axis=0, concat_axis=0, tiled=True)  4.77 us
    all_to_all x1, starting transfers between devices, routed_sums(): lax.all_to_all(stacked, 'lat', split_axis=0, concat_axis=0, tiled=True)  3.37 us
  transfers between devices with their start and end apart: 2, of which 2 were waited for; matrix products, arithmetic and copies ran while one was open for 2% of the time, Pallas kernels for 0%

profile of v1, /device:TPU:0, one launch (start us, length us, event | category | flops | bytes accessed | tf_op | source)
XLA Modules:
  0.0 75.4 jit_solution(15194445208628261132)
XLA Ops:
  0.6 0.0 copy-start
  0.6 0.8 %fusion.19 = (s32[1,128,1]{1,2,0:T(1,128)S(1)}, s32[1,128]{1,0:T(1,128)S(1)}) fusion(s32[1,128]{1,0:T(1,128)} %param.4), kind=kLoop, calls=%fused_computation.56 | loop fusion | flops 4224 | bytes 1536 | tf_op jit(solution)/shard_map/broadcast_in_dim | solution.py:24
  1.5 0.1 fusion.12
  1.6 0.2 reduce_window_sum.11
  1.7 0.2 select_reduce_fusion.2
  2.0 0.6 broadcast.449
  2.6 19.9 %scatter_fusion = s32[8,32]{1,0:T(8,128)} fusion(s32[8,32]{1,0:T(8,128)} %broadcast.449, s32[128]{0:T(128)S(1)} %fusion.21, s32[128]{0:T(128)} %bitcast.52), kind=kCustom, calls=%fused_computation.1 | custom fusion | bytes 2560 | tf_op jit(solution)/shard_map/scatter | solution.py:24
  22.4 6.4 %all-to-all-start = ((s32[8,1,32]{2,1,0:T(1,128)}), s32[8,1,32]{2,1,0:T(1,128)S(1)}, u32[]{:S(2)}, u32[]{:S(2)}) async-start(s32[8,1,32]{2,1,0:T(1,128)} %bitcast.9), calls=%async_computation | async-start | bytes 8192 | tf_op jit(solution)/shard_map/all_to_all | solution.py:27
  28.8 0.7 iota_compare_fusion.3
  29.5 4.8 %all-to-all-done = s32[8,1,32]{2,1,0:T(1,128)S(1)} async-done(((s32[8,1,32]{2,1,0:T(1,128)}), s32[8,1,32]{2,1,0:T(1,128)S(1)}, u32[]{:S(2)}, u32[]{:S(2)}) %all-to-all-start) | async-done | bytes 1056 | tf_op jit(solution)/shard_map/all_to_all | solution.py:27
  34.3 0.0 copy-done
  34.3 0.0 copy-start.1
  34.4 5.0 %fusion.7 = f32[8,1,32,128]{3,2,1,0:T(8,128)} fusion(bf16[1,8192,128]{2,1,0:T(8,128)(2,1)S(1)} %copy-done, f32[8,32]{1,0:T(8,128)S(1)} %get-tuple-element.5, s32[8,32]{1,0:T(8,128)S(1)} %get-tuple-element.6, f32[8,32]{1,0:T(8,128)S(1)} %get-tuple-element.4, s32[8,32]{1,0:T(8,128)S(1)} %get-tuple-element.7, pred[8,32]{1,0:T(8,128)(4,1)S(1)} %broadcast_compare_fusion), kind=kOutput, calls=%fused_computation.11 | convolution fusion | flops 553648128 | bytes 2232576 | tf_op jit(solution)/shard_map/dot_general | solution.py:36
  39.3 3.4 %all-to-all-start.1 = ((f32[8,1,32,128]{3,2,1,0:T(8,128)}), f32[8,1,32,128]{3,2,1,0:T(8,128)S(1)}, u32[]{:S(2)}, u32[]{:S(2)}) async-start(f32[8,1,32,128]{3,2,1,0:T(8,128)} %fusion.7), calls=%async_computation.1 | async-start | bytes 262144 | tf_op jit(solution)/shard_map/all_to_all | solution.py:39
  42.7 0.0 copy-done.1
  42.7 0.6 convert_reduce_fusion
  43.3 0.1 lt.77
  43.4 6.0 %all-to-all-done.1 = f32[8,1,32,128]{3,2,1,0:T(8,128)S(1)} async-done(((f32[8,1,32,128]{3,2,1,0:T(8,128)}), f32[8,1,32,128]{3,2,1,0:T(8,128)S(1)}, u32[]{:S(2)}, u32[]{:S(2)}) %all-to-all-start.1) | async-done | bytes 131104 | tf_op jit(solution)/shard_map/all_to_all | solution.py:39
  49.4 0.6 gather_fusion
  50.0 0.1 bitcast_select_fusion
  50.1 9.0 %all_gather.4 = f32[4,128,128]{2,1,0:T(8,128)S(1)} all-gather(f32[1,128,128]{2,1,0:T(8,128)S(1)} %bitcast_select_fusion), channel_id=1, replica_groups=mesh['seg'=4,'lat'=8] {'seg'}, dimensions={0}, use_global_device_ids=true | all-gather | bytes 327680 | tf_op jit(solution)/shard_map/all_gather | solution.py:54
  59.1 0.1 select_reduce_fusion.1
  59.2 0.6 select_reduce_fusion
  59.9 14.2 %all-reduce = (f32[128]{0:T(128)S(1)}, f32[]{:T(128)}) all-reduce(f32[128]{0:T(128)S(1)} %get-tuple-element.10, f32[]{:T(128)} %convert_reduce_fusion), channel_id=1, replica_groups=mesh['seg'=4,'lat'=8] {'lat'}, use_global_device_ids=true, to_apply=%region_6.7 | all-reduce | flops 129 | bytes 1032 | tf_op jit(solution)/shard_map/psum | solution.py:65
  74.1 0.6 broadcast_divide_fusion
  74.7 0.6 divide_subtract_fusion
  (12 shorter events, 0.1 us)
Async XLA Ops:
  0.6 33.7 %copy-start = (bf16[1,8192,128]{2,1,0:T(8,128)(2,1)S(1)}, bf16[1,8192,128]{2,1,0:T(8,128)(2,1)}, u32[]{:S(2)}) copy-start(bf16[1,8192,128]{2,1,0:T(8,128)(2,1)} %param.3) | copy-start | bytes 6291460
  22.4 11.9 %all-to-all-start = ((s32[8,1,32]{2,1,0:T(1,128)}), s32[8,1,32]{2,1,0:T(1,128)S(1)}, u32[]{:S(2)}, u32[]{:S(2)}) async-start(s32[8,1,32]{2,1,0:T(1,128)} %bitcast.9), calls=%async_computation | async-start | bytes 8192 | tf_op jit(solution)/shard_map/all_to_all | solution.py:27
  34.3 8.4 %copy-start.1 = (s32[2]{0:T(128)S(1)}, s32[2]{0:T(128)}, u32[]{:S(2)}) copy-start(s32[2]{0:T(128)} %param.5) | copy-start | bytes 28
  39.3 10.1 %all-to-all-start.1 = ((f32[8,1,32,128]{3,2,1,0:T(8,128)}), f32[8,1,32,128]{3,2,1,0:T(8,128)S(1)}, u32[]{:S(2)}, u32[]{:S(2)}) async-start(f32[8,1,32,128]{3,2,1,0:T(8,128)} %fusion.7), calls=%async_computation.1 | async-start | bytes 262144 | tf_op jit(solution)/shard_map/all_to_all | solution.py:39
